TPU v7x, 32 devices: a whole 2x2x4 slice. The times are simulated.
32 devices in a mesh: replica: 8 (over z, y), tensor: 4 (over x, core).
Axes of the slice: x: 2, y: 2, z: 4, core: 2. Of those that a mesh axis runs over, the one named last changes fastest.
Arguments:
- base_stream: bfloat16 [32, 8192], P('tensor', 'replica'), may hold values from -6 to 6
- out_weight: bfloat16 [64, 128, 8192], P('tensor', 'replica'), may hold values from -0.5 to 0.5
- queries: bfloat16 [4, 32, 64, 128], P(None, 'replica', 'tensor'), may hold values from -5 to 5
- cache_keys: bfloat16 [32, 8, 1536, 128], P('replica', 'tensor'), may hold values from -5 to 5
- cache_values: bfloat16 [32, 8, 1536, 128], P('replica', 'tensor'), may hold values from -6 to 6
- new_keys: bfloat16 [4, 32, 8, 128], P(None, 'replica', 'tensor'), may hold values from -5 to 5
- new_values: bfloat16 [4, 32, 8, 128], P(None, 'replica', 'tensor'), may hold values from -6 to 6
- lengths: int32 [32], P('replica'), may hold values from 384 to 1536
- finished: int32 [32], replicated, may hold values 0 or 1
- owners: int32 [32, 1], replicated, may hold values from 0 to 7; in each aligned block of 32 rows (0 to 31, 32 to 63, ...) at most 4 rows name the same one
Outputs:
- updates: bfloat16 [4, 32, 8192], P(None, 'tensor', 'replica')
- trainer_rows: bfloat16 [8, 4, 8192], P('replica', 'tensor')
Inputs may be any that keep to these rules, and one draw needn't show every extreme that they name: `owners`: no owner is named by more than 4 rows, and one owner is named by exactly 4.
All inputs are finite; a program needn't handle non-finite values.
Results may differ from a plain program's by a relative error of at most 0.013.
Values may be sent and summed in bfloat16 or wider, within the bound.
No kernel may reach another device: no remote copies, remote signals or barrier semaphores. Data moves between devices by JAX's collectives and lax.ppermute only.
A program may use at most 128 MiB of HBM per device.

v0:
```python
import math
import jax
import jax.numpy as jnp
from jax import lax
from jax.sharding import PartitionSpec as P

SLOT_DEV = 1


def attend(queries, cache_keys, cache_values, new_keys, new_values, lengths):
    steps_count, row_count, heads_here, head_size = queries.shape
    kv_here = cache_keys.shape[1]
    positions_count = cache_keys.shape[2]
    group_size = heads_here // kv_here
    score_scale = 1.0 / math.sqrt(head_size)
    grouped = queries.reshape(steps_count, row_count, kv_here, group_size, head_size)
    cache_scores = (
        jnp.einsum("tbgqd,bgcd->tbgqc", grouped, cache_keys, preferred_element_type=jnp.float32)
        * score_scale
    )
    positions = lax.broadcasted_iota(jnp.int32, (1, row_count, 1, 1, positions_count), 4)
    is_valid = positions < lengths[None, :, None, None, None]
    cache_scores = jnp.where(is_valid, cache_scores, jnp.float32(-1e30))
    fresh_scores = (
        jnp.einsum("tbgqd,ubgd->tbgqu", grouped, new_keys, preferred_element_type=jnp.float32)
        * score_scale
    )
    step_now = lax.broadcasted_iota(jnp.int32, (steps_count, 1, 1, 1, steps_count), 0)
    step_then = lax.broadcasted_iota(jnp.int32, (steps_count, 1, 1, 1, steps_count), 4)
    fresh_scores = jnp.where(step_then <= step_now, fresh_scores, jnp.float32(-1e30))
    highest = jnp.maximum(
        jnp.max(cache_scores, axis=-1, keepdims=True), jnp.max(fresh_scores, axis=-1, keepdims=True)
    )
    cache_weights = jnp.exp(cache_scores - highest)
    fresh_weights = jnp.exp(fresh_scores - highest)
    totals = jnp.sum(cache_weights, axis=-1, keepdims=True) + jnp.sum(
        fresh_weights, axis=-1, keepdims=True
    )
    cache_probs = (cache_weights / totals).astype(jnp.bfloat16)
    fresh_probs = (fresh_weights / totals).astype(jnp.bfloat16)
    mixed = jnp.einsum(
        "tbgqc,bgcd->tbgqd", cache_probs, cache_values, preferred_element_type=jnp.float32
    )
    mixed = mixed + jnp.einsum(
        "tbgqu,ubgd->tbgqd", fresh_probs, new_values, preferred_element_type=jnp.float32
    )
    return mixed.reshape(steps_count, row_count, heads_here * head_size).astype(jnp.bfloat16)


def reduce_heads(partial_value):
    rounded = partial_value.astype(jnp.bfloat16)
    totals = lax.psum(rounded, "tensor").astype(jnp.float32)
    share = totals.shape[1] // lax.axis_size("tensor")
    return lax.dynamic_slice_in_dim(totals, lax.axis_index("tensor") * share, share, 1)


def shards(
    base_stream,
    out_weight,
    queries,
    cache_keys,
    cache_values,
    new_keys,
    new_values,
    lengths,
    finished,
    owners,
):
    heads_here = out_weight.shape[0]
    regrouped = lax.all_to_all(out_weight, "replica", split_axis=2, concat_axis=1, tiled=True)
    weight_local = regrouped.reshape(heads_here * regrouped.shape[1], regrouped.shape[2])
    attended = attend(queries, cache_keys, cache_values, new_keys, new_values, lengths)
    partial_value = jnp.einsum(
        "tbf,fc->tbc",
        lax.all_gather(attended, "replica", axis=1, tiled=True),
        weight_local,
        preferred_element_type=jnp.float32,
    )
    summed = reduce_heads(partial_value)
    updates = summed.astype(jnp.bfloat16)
    stream = base_stream.astype(jnp.float32) + jnp.sum(updates.astype(jnp.float32), axis=0)
    stream_rounded = stream.astype(jnp.bfloat16)
    all_streams = lax.all_gather(stream_rounded, "tensor", axis=0, tiled=True)
    owner_count = lax.axis_size("replica")
    owner_ids = lax.broadcasted_iota(jnp.int32, (1, owner_count), 1)
    onehot = (owners == owner_ids).astype(jnp.int32)
    before = jnp.cumsum(onehot, axis=0) - onehot
    slot_rank = jnp.sum(before * onehot, axis=1)
    first_slot = lax.axis_index("tensor") * SLOT_DEV
    slot_ids = first_slot + lax.broadcasted_iota(jnp.int32, (1, 1, SLOT_DEV), 2)
    chosen = (
        onehot[:, :, None]
        * (slot_rank[:, None, None] == slot_ids).astype(jnp.int32)
        * finished[:, None, None]
    )
    selector = chosen.astype(jnp.bfloat16)
    outgoing = jnp.einsum(
        "jos,jc->osc", selector, all_streams, preferred_element_type=jnp.float32
    ).astype(jnp.bfloat16)
    trainer_rows = lax.all_to_all(outgoing, "replica", split_axis=0, concat_axis=2, tiled=True)
    return (updates, trainer_rows)


def solution(mesh):
    placed = (
        P("tensor", "replica"),
        P("tensor", "replica", None),
        P(None, "replica", "tensor", None),
        P("replica", "tensor", None, None),
        P("replica", "tensor", None, None),
        P(None, "replica", "tensor", None),
        P(None, "replica", "tensor", None),
        P("replica"),
        P(),
        P(),
    )
    return jax.shard_map(
        shards,
        mesh=mesh,
        in_specs=placed,
        out_specs=(P(None, "tensor", "replica"), P("replica", "tensor", None)),
        check_vma=False,
    )
```

profile of v0, /device:TPU:0, one launch (start us, length us, event | category | flops | bytes accessed | tf_op | source)
XLA Modules:
  0.0 318.9 jit_solution(999825138677871653)
XLA Ops:
  7.2 0.0 copy-start
  7.2 27.8 %copy.29 = bf16[16,16,8192]{1,0,2:T(8,128)(2,1)} copy(bf16[16,16,8192]{2,1,0:T(8,128)(2,1)} %param.11) | data formatting | bytes 8388608 | tf_op args[1]
  35.0 37.7 %reshape.116 = bf16[8,2,131072]{2,1,0:T(2,128)(2,1)} reshape(bf16[8192,16,16]{2,1,0:T(8,128)(2,1)} %bitcast.60) | data formatting | bytes 8388608
  72.7 0.0 copy-start.2
  72.7 0.0 copy-start.7
  72.7 0.0 copy-start.5
  72.7 7.4 %all-to-all-start = ((bf16[8,2,131072]{2,1,0:T(2,128)(2,1)}), bf16[8,2,131072]{2,1,0:T(2,128)(2,1)}, u32[]{:S(2)}, u32[]{:S(2)}) async-start(bf16[8,2,131072]{2,1,0:T(2,128)(2,1)} %reshape.116), calls=%async_computation | async-start | bytes 8388608 | tf_op jit(solution)/shard_map/all_to_all | solution.py:70
  80.2 0.0 all-reduce.2.cloned.1.call-start
  80.2 0.0 copy-done.2
  80.2 0.0 copy-done.7
  80.2 0.4 fusion.44
  80.7 0.0 copy-done.5
  80.7 0.1 iota_compare_fusion
  80.8 0.0 copy-done
  80.8 0.0 copy-start.8
  80.8 0.0 copy-start.6
  80.8 1.2 fusion.43
  82.0 0.1 fusion.31
  82.1 0.4 fusion.13
  82.5 0.0 copy-done.8
  82.5 0.2 fusion.32
  82.7 0.0 copy-done.6
  82.7 0.0 copy-start.4
  82.7 0.7 fusion.20
  83.5 0.0 copy-done.4
  83.5 0.1 fusion.35
  83.6 0.1 reduce_window_sum.11
  83.6 0.2 select_reduce_fusion
  83.8 112.7 %all_gather.6 = bf16[4,32,2048]{2,0,1:T(4,128)(2,1)} all-gather(bf16[4,4,2048]{2,0,1:T(4,128)(2,1)S(1)} %reshape.115), channel_id=1, replica_groups=mesh['replica'=8,'tensor'=4] {'replica'}, dimensions={1}, use_global_device_ids=true | all-gather | bytes 589824 | tf_op jit(solution)/shard_map/all_gather | solution.py:75
  196.5 0.0 all-to-all-done
  196.5 25.8 %reshape.117 = bf16[8192,16,16]{2,1,0:T(8,128)(2,1)} reshape(bf16[8,2,131072]{2,1,0:T(2,128)(2,1)} %all-to-all-done) | data formatting | bytes 8388608
  222.3 32.9 %copy.30 = bf16[16,16,8,1024]{3,1,2,0:T(8,128)(2,1)} copy(bf16[16,16,8,1024]{1,0,3,2:T(8,128)(2,1)} %bitcast.59) | data formatting | bytes 8388608 | tf_op jit(solution)/shard_map/all_to_all | solution.py:70
  255.2 0.0 copy-start.1
  255.2 0.0 copy-start.3
  255.2 0.0 copy-start.9
  255.2 4.2 %convolution_convert_fusion = bf16[4,32,1024]{2,1,0:T(8,128)(2,1)} fusion(bf16[2048,1024,1]{1,0,2:T(8,128)(2,1)} %bitcast.61, bf16[4,32,2048]{2,0,1:T(4,128)(2,1)} %all_gather.6), kind=kOutput, calls=%fused_computation.10 | convolution fusion | flops 537001984 | bytes 4980736 | tf_op jit(solution)/shard_map/tbf,fc->tbc/dot_general | solution.py:73
  259.4 0.0 all-reduce.2.cloned.1.call-update
  259.5 31.9 %all-reduce.2.cloned.1.call-done = bf16[4,32,1024]{2,1,0:T(8,128)(2,1)} async-done(((bf16[4,32,1024]{2,1,0:T(8,128)(2,1)}), bf16[4,32,1024]{2,1,0:T(8,128)(2,1)}) %all-reduce.2.cloned.1.call-update) | async-done | bytes 262160 | tf_op jit(solution)/shard_map/psum | solution.py:52
  291.3 1.5 convert_reduce_fusion
  292.8 0.0 copy-done.3
  292.8 5.2 %all_gather.7 = bf16[32,1024]{1,0:T(8,128)(2,1)S(1)} all-gather(bf16[8,1024]{1,0:T(8,128)(2,1)S(1)} %add_convert_fusion), channel_id=1, replica_groups=mesh['replica'=8,'tensor'=4] {'tensor'}, dimensions={0}, use_global_device_ids=true | all-gather | bytes 81920 | tf_op jit(solution)/shard_map/all_gather | solution.py:83
  298.1 0.0 copy-done.9
  298.1 0.3 fusion.25
  298.3 0.5 broadcast.58
  298.9 0.7 reduce
  299.5 11.9 %all_to_all.27 = bf16[8,2,512]{2,1,0:T(2,128)(2,1)S(1)} all-to-all(bf16[8,2,512]{2,1,0:T(2,128)(2,1)S(1)} %reshape.118), channel_id=1, replica_groups=mesh['replica'=8,'tensor'=4] {'replica'}, dimensions={0} | all-to-all | bytes 32768 | tf_op jit(solution)/shard_map/all_to_all | solution.py:100
  311.4 0.6 reshape.119
  312.1 0.0 copy-done.1
  (8 shorter events, 0.1 us)
Async XLA Ops:
  7.2 73.6 %copy-start = (bf16[4,2,1536,128]{3,2,1,0:T(8,128)(2,1)S(1)}, bf16[4,2,1536,128]{3,2,1,0:T(8,128)(2,1)}, u32[]{:S(2)}) copy-start(bf16[4,2,1536,128]{3,2,1,0:T(8,128)(2,1)} %param.13) | copy-start | bytes 9437188
  72.7 7.5 %copy-start.2 = (bf16[4,4,16,128]{3,2,1,0:T(8,128)(2,1)S(1)}, bf16[4,4,16,128]{3,2,1,0:T(8,128)(2,1)}, u32[]{:S(2)}) copy-start(bf16[4,4,16,128]{3,2,1,0:T(8,128)(2,1)} %param.12) | copy-start | bytes 196612
  72.7 7.5 %copy-start.7 = (bf16[4,4,2,128]{3,2,1,0:T(2,128)(2,1)S(1)}, bf16[4,4,2,128]{3,2,1,0:T(2,128)(2,1)}, u32[]{:S(2)}) copy-start(bf16[4,4,2,128]{3,2,1,0:T(2,128)(2,1)} %param.15) | copy-start | bytes 24580
  72.7 8.0 %copy-start.5 = (s32[4]{0:T(128)S(1)}, s32[4]{0:T(128)}, u32[]{:S(2)}) copy-start(s32[4]{0:T(128)} %param.17) | copy-start | bytes 52
  72.7 123.8 %all-to-all-start = ((bf16[8,2,131072]{2,1,0:T(2,128)(2,1)}), bf16[8,2,131072]{2,1,0:T(2,128)(2,1)}, u32[]{:S(2)}, u32[]{:S(2)}) async-start(bf16[8,2,131072]{2,1,0:T(2,128)(2,1)} %reshape.116), calls=%async_computation | async-start | bytes 8388608 | tf_op jit(solution)/shard_map/all_to_all | solution.py:70
  80.2 211.2 %all-reduce.2.cloned.1.call-start = ((), (), s32[]{:S(2)}) async-start(), calls=%async_computation.2 | async-start | bytes 524288 | tf_op jit(solution)/shard_map/psum | solution.py:52
  80.8 1.7 copy-start.8
  80.8 1.9 copy-start.6
  82.7 0.8 copy-start.4
  255.2 56.9 %copy-start.1 = (bf16[4,2,1536,128]{3,2,1,0:T(8,128)(2,1)S(1)}, bf16[4,2,1536,128]{3,2,1,0:T(8,128)(2,1)}, u32[]{:S(2)}) copy-start(bf16[4,2,1536,128]{3,2,1,0:T(8,128)(2,1)} %param.13) | copy-start | bytes 9437188
  255.2 37.6 %copy-start.3 = (bf16[8,1024]{1,0:T(8,128)(2,1)S(1)}, bf16[8,1024]{1,0:T(8,128)(2,1)}, u32[]{:S(2)}) copy-start(bf16[8,1024]{1,0:T(8,128)(2,1)} %param.10) | copy-start | bytes 49156
  255.2 42.9 %copy-start.9 = (s32[32]{0:T(128)S(1)}, s32[32]{0:T(128)}, u32[]{:S(2)}) copy-start(s32[32]{0:T(128)} %param.18) | copy-start | bytes 388
Sparse Core Ops, SparseCore 0:
  259.6 31.7 all-reduce.1
where the time goes:
time: 321 us; the launch traced here: 319 us
  blocking collectives  130 us (40%)
  local copies, waits for them, and re-layouts  125 us (39%)
  waiting for transfers between devices  31.9 us (10%)
  between operations  14.2 us (4%)
  starting transfers between devices  7.48 us (2%)
  matrix products  7.07 us (2%)
    all_gather x1, blocking collectives, shards(): lax.all_gather(attended, 'replica', axis=1, tiled=True)  113 us
    unnamed x25, local copies, waits for them, and re-layouts  92 us
    all_to_all x1, local copies, waits for them, and re-layouts, shards(): lax.all_to_all(out_weight, 'replica', split_axis=2, concat_axis=1, tiled=...  32.9 us
    psum x1, waiting for transfers between devices, reduce_heads(): totals = lax.psum(rounded, 'tensor').astype(jnp.float32)  31.9 us
    all_to_all x1, blocking collectives, shards(): lax.all_to_all(outgoing, 'replica', split_axis=0, concat_axis=2, tiled=True)  11.9 us
    all_to_all x1, starting transfers between devices, shards(): lax.all_to_all(out_weight, 'replica', split_axis=2, concat_axis=1, tiled=...  7.45 us
  transfers between devices with their start and end apart: 2, of which 1 were waited for; matrix products, arithmetic and copies ran while one was open for 1% of the time, Pallas kernels for 0%

commit v1 on v0

--- a/solution.py
+++ b/solution.py
@@ -49,7 +49,7 @@
 
 def reduce_heads(partial_value):
     rounded = partial_value.astype(jnp.bfloat16)
-    totals = lax.psum(rounded, "tensor").astype(jnp.float32)
+    totals = jnp.sum(lax.all_gather(rounded, "tensor"), axis=0).astype(jnp.float32)
     share = totals.shape[1] // lax.axis_size("tensor")
     return lax.dynamic_slice_in_dim(totals, lax.axis_index("tensor") * share, share, 1)
 

time: 321 us -> 306 us (0.953)
  waiting for transfers between devices: 31.9 us -> 16 us
    psum x1 -> x0, waiting for transfers between devices: 31.9 us -> none  [reduce_heads(): totals = lax.psum(rounded, 'tensor').astype(jnp.float32)]
    all_gather x0 -> x1, waiting for transfers between devices: none -> 16 us  [reduce_heads(): lax.all_gather(rounded, 'tensor')]
where the time goes in v1:
time: 306 us; the launch traced here: 304 us
  blocking collectives  130 us (42%)
  local copies, waits for them, and re-layouts  125 us (41%)
  waiting for transfers between devices  16 us (5%)
  between operations  14.2 us (5%)
  starting transfers between devices  7.49 us (2%)
  matrix products  7.08 us (2%)
  other arithmetic  3.59 us (1%)
    all_gather x1, blocking collectives, shards(): lax.all_gather(attended, 'replica', axis=1, tiled=True)  113 us
    unnamed x25, local copies, waits for them, and re-layouts  92 us
    all_to_all x1, local copies, waits for them, and re-layouts, shards(): lax.all_to_all(out_weight, 'replica', split_axis=2, concat_axis=1, tiled=...  32.9 us
    all_gather x1, waiting for transfers between devices, reduce_heads(): lax.all_gather(rounded, 'tensor')  16 us
    all_to_all x1, blocking collectives, shards(): lax.all_to_all(outgoing, 'replica', split_axis=0, concat_axis=2, tiled=True)  11.9 us
    all_to_all x1, starting transfers between devices, shards(): lax.all_to_all(out_weight, 'replica', split_axis=2, concat_axis=1, tiled=...  7.45 us
  transfers between devices with their start and end apart: 2, of which 1 were waited for; matrix products, arithmetic and copies ran while one was open for 1% of the time, Pallas kernels for 0%

profile of v1, /device:TPU:0, one launch (start us, length us, event | category | flops | bytes accessed | tf_op | source)
XLA Modules:
  0.0 303.9 jit_solution(15393141523697731162)
XLA Ops:
  7.2 0.0 copy-start
  7.2 27.8 %copy.29 = bf16[16,16,8192]{1,0,2:T(8,128)(2,1)} copy(bf16[16,16,8192]{2,1,0:T(8,128)(2,1)} %param.11) | data formatting | bytes 8388608 | tf_op args[1]
  35.0 37.7 %reshape.117 = bf16[8,2,131072]{2,1,0:T(2,128)(2,1)} reshape(bf16[8192,16,16]{2,1,0:T(8,128)(2,1)} %bitcast.61) | data formatting | bytes 8388608
  72.7 0.0 copy-start.2
  72.7 0.0 copy-start.7
  72.7 0.0 copy-start.5
  72.7 7.4 %all-to-all-start = ((bf16[8,2,131072]{2,1,0:T(2,128)(2,1)}), bf16[8,2,131072]{2,1,0:T(2,128)(2,1)}, u32[]{:S(2)}, u32[]{:S(2)}) async-start(bf16[8,2,131072]{2,1,0:T(2,128)(2,1)} %reshape.117), calls=%async_computation | async-start | bytes 8388608 | tf_op jit(solution)/shard_map/all_to_all | solution.py:70
  80.2 0.0 all-gather.3.cloned.1.call-start
  80.2 0.0 copy-done.2
  80.2 0.0 copy-done.7
  80.2 0.4 fusion.44
  80.7 0.0 copy-done.5
  80.7 0.1 iota_compare_fusion
  80.8 0.0 copy-done
  80.8 0.0 copy-start.8
  80.8 0.0 copy-start.6
  80.8 1.2 fusion.43
  82.0 0.1 fusion.31
  82.1 0.4 fusion.13
  82.5 0.0 copy-done.8
  82.5 0.2 fusion.32
  82.7 0.0 copy-done.6
  82.7 0.7 fusion.20
  83.5 113.1 %all_gather.12 = bf16[4,32,2048]{2,0,1:T(4,128)(2,1)} all-gather(bf16[4,4,2048]{2,0,1:T(4,128)(2,1)S(1)} %reshape.116), channel_id=1, replica_groups=mesh['replica'=8,'tensor'=4] {'replica'}, dimensions={1}, use_global_device_ids=true | all-gather | bytes 589824 | tf_op jit(solution)/shard_map/all_gather | solution.py:75
  196.5 0.0 all-to-all-done
  196.5 25.8 %reshape.118 = bf16[8192,16,16]{2,1,0:T(8,128)(2,1)} reshape(bf16[8,2,131072]{2,1,0:T(2,128)(2,1)} %all-to-all-done) | data formatting | bytes 8388608
  222.3 32.9 %copy.30 = bf16[16,16,8,1024]{3,1,2,0:T(8,128)(2,1)} copy(bf16[16,16,8,1024]{1,0,3,2:T(8,128)(2,1)} %bitcast.60) | data formatting | bytes 8388608 | tf_op jit(solution)/shard_map/all_to_all | solution.py:70
  255.2 0.0 copy-start.1
  255.2 0.0 copy-start.4
  255.2 0.0 copy-start.3
  255.2 4.2 %convolution_convert_fusion = bf16[4,32,1024]{2,1,0:T(8,128)(2,1)} fusion(bf16[2048,1024,1]{1,0,2:T(8,128)(2,1)} %bitcast.62, bf16[4,32,2048]{2,0,1:T(4,128)(2,1)} %all_gather.12), kind=kOutput, calls=%fused_computation.10 | convolution fusion | flops 537001984 | bytes 4980736 | tf_op jit(solution)/shard_map/tbf,fc->tbc/dot_general | solution.py:73
  259.4 0.0 all-gather.3.cloned.1.call-update
  259.5 0.0 copy-done.4
  259.5 0.1 fusion.35
  259.6 0.1 reduce_window_sum.11
  259.6 0.2 select_reduce_fusion
  259.8 16.0 %all-gather.3.cloned.1.call-done = bf16[16,32,1024]{2,1,0:T(8,128)(2,1)} async-done(((bf16[4,32,1024]{2,1,0:T(8,128)(2,1)}), bf16[16,32,1024]{2,1,0:T(8,128)(2,1)}) %all-gather.3.cloned.1.call-update) | async-done | bytes 1048592 | tf_op jit(solution)/shard_map/all_gather | solution.py:52
  275.8 1.4 reduce_sum.50
  277.2 0.6 convert_reduce_fusion
  277.9 0.0 copy-done.3
  277.9 5.2 %all_gather.15 = bf16[32,1024]{1,0:T(8,128)(2,1)S(1)} all-gather(bf16[8,1024]{1,0:T(8,128)(2,1)S(1)} %add_convert_fusion), channel_id=1, replica_groups=mesh['replica'=8,'tensor'=4] {'tensor'}, dimensions={0}, use_global_device_ids=true | all-gather | bytes 81920 | tf_op jit(solution)/shard_map/all_gather | solution.py:83
  283.1 0.0 copy-done.9
  283.1 0.3 fusion.25
  283.4 0.5 broadcast.58
  283.9 0.7 reduce.1
  284.6 11.9 %all_to_all.27 = bf16[8,2,512]{2,1,0:T(2,128)(2,1)S(1)} all-to-all(bf16[8,2,512]{2,1,0:T(2,128)(2,1)S(1)} %reshape.119), channel_id=1, replica_groups=mesh['replica'=8,'tensor'=4] {'replica'}, dimensions={0} | all-to-all | bytes 32768 | tf_op jit(solution)/shard_map/all_to_all | solution.py:100
  296.5 0.6 reshape.120
  297.1 0.0 copy-done.1
  (9 shorter events, 0.1 us)
Async XLA Ops:
  7.2 73.6 %copy-start = (bf16[4,2,1536,128]{3,2,1,0:T(8,128)(2,1)S(1)}, bf16[4,2,1536,128]{3,2,1,0:T(8,128)(2,1)}, u32[]{:S(2)}) copy-start(bf16[4,2,1536,128]{3,2,1,0:T(8,128)(2,1)} %param.13) | copy-start | bytes 9437188
  72.7 7.5 %copy-start.2 = (bf16[4,4,16,128]{3,2,1,0:T(8,128)(2,1)S(1)}, bf16[4,4,16,128]{3,2,1,0:T(8,128)(2,1)}, u32[]{:S(2)}) copy-start(bf16[4,4,16,128]{3,2,1,0:T(8,128)(2,1)} %param.12) | copy-start | bytes 196612
  72.7 7.5 %copy-start.7 = (bf16[4,4,2,128]{3,2,1,0:T(2,128)(2,1)S(1)}, bf16[4,4,2,128]{3,2,1,0:T(2,128)(2,1)}, u32[]{:S(2)}) copy-start(bf16[4,4,2,128]{3,2,1,0:T(2,128)(2,1)} %param.15) | copy-start | bytes 24580
  72.7 8.0 %copy-start.5 = (s32[4]{0:T(128)S(1)}, s32[4]{0:T(128)}, u32[]{:S(2)}) copy-start(s32[4]{0:T(128)} %param.17) | copy-start | bytes 52
  72.7 123.8 %all-to-all-start = ((bf16[8,2,131072]{2,1,0:T(2,128)(2,1)}), bf16[8,2,131072]{2,1,0:T(2,128)(2,1)}, u32[]{:S(2)}, u32[]{:S(2)}) async-start(bf16[8,2,131072]{2,1,0:T(2,128)(2,1)} %reshape.117), calls=%async_computation | async-start | bytes 8388608 | tf_op jit(solution)/shard_map/all_to_all | solution.py:70
  80.2 195.6 %all-gather.3.cloned.1.call-start = ((), (), s32[]{:S(2)}) async-start(), calls=%async_computation.2 | async-start | bytes 1310720 | tf_op jit(solution)/shard_map/all_gather | solution.py:52
  80.8 1.7 copy-start.8
  80.8 1.9 copy-start.6
  255.2 41.9 %copy-start.1 = (bf16[4,2,1536,128]{3,2,1,0:T(8,128)(2,1)S(1)}, bf16[4,2,1536,128]{3,2,1,0:T(8,128)(2,1)}, u32[]{:S(2)}) copy-start(bf16[4,2,1536,128]{3,2,1,0:T(8,128)(2,1)} %param.13) | copy-start | bytes 9437188
  255.2 4.3 %copy-start.4 = (s32[32,1]{0,1:T(1,128)S(1)}, s32[32,1]{0,1:T(1,128)}, u32[]{:S(2)}) copy-start(s32[32,1]{0,1:T(1,128)} %param.19) | copy-start | bytes 388
  255.2 22.7 %copy-start.3 = (bf16[8,1024]{1,0:T(8,128)(2,1)S(1)}, bf16[8,1024]{1,0:T(8,128)(2,1)}, u32[]{:S(2)}) copy-start(bf16[8,1024]{1,0:T(8,128)(2,1)} %param.10) | copy-start | bytes 49156
  255.2 27.9 %copy-start.9 = (s32[32]{0:T(128)S(1)}, s32[32]{0:T(128)}, u32[]{:S(2)}) copy-start(s32[32]{0:T(128)} %param.18) | copy-start | bytes 388
Sparse Core Ops, SparseCore 0:
  259.6 16.1 all-gather.2
